TPU v7x, 32 devices: a 4x4x1 block of a 4x4x8 slice. The times are simulated.
32 devices in a mesh: dp: 1 (over z), fsdp: 32 (over y, x, core).
Axes of the slice: x: 4, y: 4, z: 1, core: 2. Of those that a mesh axis runs over, the one named last changes fastest.
The devices are a block of a 4x4x8 slice.
Arguments:
- tok_ids: int32 [96, 96], P(('dp', 'fsdp'))
- grad_out: bfloat16 [96, 96, 2048], P(('dp', 'fsdp'))
- emb_table: bfloat16 [163840, 2048], P('fsdp')
- norm_gain: bfloat16 [2048], P('fsdp')
- w_query: bfloat16 [2048, 3072], P('fsdp')
- w_kv_down: bfloat16 [2048, 576], P('fsdp')
- kv_gain: bfloat16 [512], P('fsdp')
- w_kv_up: bfloat16 [512, 4096], P('fsdp')
- w_out: bfloat16 [2048, 2048], P('fsdp')
Outputs:
- output 1: bfloat16 [96, 96, 2048], P(('dp', 'fsdp'))
- output 2: bfloat16 [163840, 2048], P(('dp', 'fsdp'))
- output 3: float32 [2048], P(('dp', 'fsdp'))
- output 4: float32 [2048, 3072], P(('dp', 'fsdp'))
- output 5: float32 [2048, 576], P(('dp', 'fsdp'))
- output 6: float32 [512], P(('dp', 'fsdp'))
- output 7: float32 [512, 4096], P(('dp', 'fsdp'))
- output 8: float32 [2048, 2048], P(('dp', 'fsdp'))
All inputs are finite; a program needn't handle non-finite values.
Results may differ from a plain program's by a relative error of at most 0.0116745.
Values are sent between devices in bfloat16 or wider.
A program may use at most 768 MiB of HBM per device.

v0:
```python
import math
import jax
import jax.numpy as jnp
from jax import lax
from jax.sharding import PartitionSpec as P

NOPE_DIM = 128
ROPE_DIM = 64
VALUE_DIM = 128
ROPE_THETA = 50000.0
RMS_EPS = 1e-6
ATTN_SCALE = (NOPE_DIM + ROPE_DIM) ** -0.5 * (0.1 * math.log(32.0) + 1.0) ** 2
ROW_DIMS = (((0,), (0,)), ((), ()))
COL_DIMS = (((1,), (1,)), ((), ()))


def rms_scale(in_vals, gain_vec):
    vals_f32 = in_vals.astype(jnp.float32)
    inv_rms = lax.rsqrt(jnp.mean(vals_f32 * vals_f32, axis=-1, keepdims=True) + RMS_EPS)
    return (vals_f32 * inv_rms * gain_vec).astype(jnp.bfloat16)


def rope_tables(seq_len):
    positions = jnp.arange(seq_len, dtype=jnp.float32)
    inv_freq = ROPE_THETA ** (-2.0 * jnp.arange(ROPE_DIM // 2, dtype=jnp.float32) / ROPE_DIM)
    rot_angle = positions[:, None] * inv_freq[None, :]
    rot_angle = jnp.concatenate([rot_angle, rot_angle], axis=-1)
    return jnp.cos(rot_angle), jnp.sin(rot_angle)


def apply_rope(in_vals, cos_tab, sin_tab):
    half_dim = ROPE_DIM // 2
    vals_f32 = in_vals.astype(jnp.float32)
    turned = jnp.concatenate([-vals_f32[..., half_dim:], vals_f32[..., :half_dim]], axis=-1)
    return (vals_f32 * cos_tab + turned * sin_tab).astype(jnp.bfloat16)


def attend_local(q_proj, pe_raw, kv_up):
    seq_len = q_proj.shape[1]
    cos_tab, sin_tab = rope_tables(seq_len)
    q_rot = apply_rope(q_proj[..., NOPE_DIM:], cos_tab[:, None, :], sin_tab[:, None, :])
    k_rot = apply_rope(pe_raw, cos_tab, sin_tab)
    scores = jnp.einsum('bshd,bthd->bhst', q_proj[..., :NOPE_DIM], kv_up[..., :NOPE_DIM], preferred_element_type=jnp.float32)
    scores = scores + jnp.einsum('bshd,btd->bhst', q_rot, k_rot, preferred_element_type=jnp.float32)
    positions = jnp.arange(seq_len)
    causal = positions[:, None] >= positions[None, :]
    scores = jnp.where(causal, scores * ATTN_SCALE, -1e30)
    attn_probs = jax.nn.softmax(scores, axis=-1).astype(jnp.bfloat16)
    attn_mix = jnp.einsum('bhst,bthd->bshd', attn_probs, kv_up[..., NOPE_DIM:], preferred_element_type=jnp.float32)
    return attn_mix.astype(jnp.bfloat16)


def block_step(tok_rows, grad_rows, full_weights, seq_count):
    gain_vec, w_query, w_kv_down, kv_gain, w_kv_up, w_out = full_weights
    kv_rank = kv_gain.shape[0]
    tok_count = tok_rows.shape[0]
    seq_len = tok_count // seq_count
    rows_f32 = tok_rows.astype(jnp.float32)
    normed, norm_pull = jax.vjp(rms_scale, rows_f32, gain_vec.astype(jnp.float32))
    q_proj = jnp.dot(normed, w_query, preferred_element_type=jnp.float32).astype(jnp.bfloat16)
    kv_down = jnp.dot(normed, w_kv_down, preferred_element_type=jnp.float32).astype(jnp.bfloat16)
    latent, latent_pull = jax.vjp(rms_scale, kv_down[:, :kv_rank], kv_gain.astype(jnp.float32))
    kv_up = jnp.dot(latent, w_kv_up, preferred_element_type=jnp.float32).astype(jnp.bfloat16)
    attn_mix, attn_pull = jax.vjp(attend_local, q_proj.reshape(seq_count, seq_len, -1, NOPE_DIM + ROPE_DIM), kv_down[:, kv_rank:].reshape(seq_count, seq_len, ROPE_DIM), kv_up.reshape(seq_count, seq_len, -1, NOPE_DIM + VALUE_DIM))
    mix_rows = attn_mix.reshape(tok_count, -1)
    out_f32 = rows_f32 + jnp.dot(mix_rows, w_out, preferred_element_type=jnp.float32)
    d_w_out = lax.dot_general(mix_rows, grad_rows, ROW_DIMS, preferred_element_type=jnp.float32)
    d_mix = lax.dot_general(grad_rows, w_out, COL_DIMS, preferred_element_type=jnp.float32).astype(jnp.bfloat16)
    d_query, d_pe, d_up = attn_pull(d_mix.reshape(attn_mix.shape))
    d_query = d_query.reshape(tok_count, -1)
    d_up = d_up.reshape(tok_count, -1)
    d_w_kv_up = lax.dot_general(latent, d_up, ROW_DIMS, preferred_element_type=jnp.float32)
    d_latent = lax.dot_general(d_up, w_kv_up, COL_DIMS, preferred_element_type=jnp.float32).astype(jnp.bfloat16)
    d_ckv, d_kv_gain = latent_pull(d_latent)
    d_down = jnp.concatenate([d_ckv, d_pe.reshape(tok_count, ROPE_DIM)], axis=1)
    d_w_kv_down = lax.dot_general(normed, d_down, ROW_DIMS, preferred_element_type=jnp.float32)
    d_w_query = lax.dot_general(normed, d_query, ROW_DIMS, preferred_element_type=jnp.float32)
    d_normed = lax.dot_general(d_query, w_query, COL_DIMS, preferred_element_type=jnp.float32)
    d_normed = d_normed + lax.dot_general(d_down, w_kv_down, COL_DIMS, preferred_element_type=jnp.float32)
    d_rows, d_gain = norm_pull(d_normed.astype(jnp.bfloat16))
    d_rows = d_rows + grad_rows.astype(jnp.float32)
    return out_f32.astype(jnp.bfloat16), d_rows, (d_gain, d_w_query, d_w_kv_down, d_kv_gain, d_w_kv_up, d_w_out)


def solution(mesh):
    tok_spec = P(('dp', 'fsdp'), None)
    seq_spec = P(('dp', 'fsdp'), None, None)
    part_vec = P(('dp', 'fsdp'))
    vec_spec = P('fsdp')
    mat_spec = P('fsdp', None)

    def device_step(tok_ids, grad_out, emb_table, norm_gain, w_query, w_kv_down, kv_gain, w_kv_up, w_out):
        seq_count, seq_len = tok_ids.shape
        vocab_dev, d_model = emb_table.shape
        tok_count = seq_count * seq_len
        all_ids = lax.all_gather(tok_ids.reshape(tok_count), 'fsdp', tiled=True)
        local_ids = all_ids - lax.axis_index('fsdp') * vocab_dev
        is_owned = (local_ids >= 0) & (local_ids < vocab_dev)
        picked = jnp.take(emb_table, jnp.where(is_owned, local_ids, 0), axis=0)
        picked = jnp.where(is_owned[:, None], picked, jnp.zeros((), picked.dtype))
        tok_rows = lax.psum_scatter(picked, 'fsdp', scatter_dimension=0, tiled=True)
        full_weights = tuple(lax.all_gather(shard_piece, 'fsdp', tiled=True) for shard_piece in (norm_gain, w_query, w_kv_down, kv_gain, w_kv_up, w_out))
        block_out, d_rows, weight_grads = block_step(tok_rows, grad_out.reshape(tok_count, d_model), full_weights, seq_count)
        all_grads = lax.all_gather(d_rows, 'fsdp', tiled=True)
        seg_ids = jnp.where(is_owned, local_ids, vocab_dev)
        grad_table = jax.ops.segment_sum(all_grads, seg_ids, num_segments=vocab_dev).astype(jnp.bfloat16)
        grad_shards = tuple(lax.psum_scatter(full_grad, 'fsdp', scatter_dimension=0, tiled=True) for full_grad in weight_grads)
        return (block_out.reshape(seq_count, seq_len, d_model), grad_table) + grad_shards

    return jax.shard_map(device_step, mesh=mesh, in_specs=(tok_spec, seq_spec, mat_spec, vec_spec, mat_spec, mat_spec, vec_spec, mat_spec, mat_spec), out_specs=(seq_spec, tok_spec, part_vec, tok_spec, tok_spec, part_vec, tok_spec, tok_spec), check_vma=False)
```

profile of v0, /device:TPU:97, one launch (start us, length us, event | category | flops | bytes accessed | tf_op | source)
XLA Modules:
  0.0 1169.2 jit_solution(7717400564313821868)
XLA Ops:
  9.1 51.2 %all-reduce.8 = s32[9216]{0:T(1024)S(1)} all-reduce(s32[9216]{0:T(1024)S(1)} %dynamic-update-slice), channel_id=1, replica_groups=mesh['dp'=1,'fsdp'=32] {'fsdp'}, use_global_device_ids=true, to_apply=%add.8 | all-reduce | flops 9216 | bytes 73728
  60.9 78.5 %gather_fusion = bf16[9216,2048]{1,0:T(8,128)(2,1)} fusion(bf16[5120,2048]{1,0:T(8,128)(2,1)} %param.11, s32[9216]{0:T(1024)S(1)} %get-tuple-element.31), kind=kCustom, calls=%fused_computation | custom fusion | bytes 75534336 | tf_op jit(solution)/shard_map/jit(_take)/gather | solution.py:99
  139.4 25.6 %select_select_fusion = bf16[9216,2048]{1,0:T(8,128)(2,1)} fusion(bf16[9216,2048]{1,0:T(8,128)(2,1)} %gather_fusion, pred[9216]{0:T(1024)(128)(4,1)S(1)} %get-tuple-element.33, pred[9216]{0:T(1024)(128)(4,1)S(1)} %get-tuple-element.32), kind=kLoop, calls=%fused_computation.2 | loop fusion | flops 37748736 | bytes 75515904 | tf_op jit(solution)/shard_map/jit(_where)/select_n | solution.py:100
  167.8 44.0 %all-reduce.14 = (bf16[512]{0:T(512)(128)(2,1)S(1)}, bf16[2048]{0:T(1024)(128)(2,1)S(1)}) all-reduce(bf16[512]{0:T(512)(128)(2,1)S(1)} %dynamic-update-slice.2, bf16[2048]{0:T(1024)(128)(2,1)S(1)} %dynamic-update-slice.1), channel_id=1, replica_groups=mesh['dp'=1,'fsdp'=32] {'fsdp'}, use_global_device_ids=true, to_apply=%add.10 | all-reduce | flops 2560 | bytes 10240
  214.8 6.0 fusion.38
  222.1 111.4 %reduce-scatter.6.cloned.1.call-done = bf16[288,2048]{1,0:T(8,128)(2,1)} async-done(((bf16[9216,2048]{1,0:T(8,128)(2,1)}), bf16[288,2048]{1,0:T(8,128)(2,1)}) %reduce-scatter.6.cloned.1.call-update) | async-done | bytes 1179664 | tf_op jit(solution)/shard_map/reduce_scatter | solution.py:101
  335.7 57.5 %all-gather.10.cloned.1.call-done = bf16[2048,3072]{1,0:T(8,128)(2,1)} async-done(((bf16[64,3072]{1,0:T(8,128)(2,1)}), bf16[2048,3072]{1,0:T(8,128)(2,1)}) %all-gather.10.cloned.1.call-update) | async-done | bytes 12582928 | tf_op jit(solution)/shard_map/all_gather | solution.py:102
  393.2 10.1 convolution_convert_fusion.1
  403.3 4.2 reshape.193
  410.0 23.6 %all-gather.6.cloned.1.call-done = bf16[2048,576]{1,0:T(8,128)(2,1)} async-done(((bf16[64,576]{1,0:T(8,128)(2,1)}), bf16[2048,576]{1,0:T(8,128)(2,1)}) %all-gather.6.cloned.1.call-update) | async-done | bytes 2359312 | tf_op jit(solution)/shard_map/all_gather | solution.py:102
  439.6 36.2 %all-gather.8.cloned.1.call-done = bf16[512,4096]{1,0:T(8,128)(2,1)} async-done(((bf16[16,4096]{1,0:T(8,128)(2,1)}), bf16[512,4096]{1,0:T(8,128)(2,1)}) %all-gather.8.cloned.1.call-update) | async-done | bytes 4194320 | tf_op jit(solution)/shard_map/all_gather | solution.py:102
  516.2 8.0 fusion.93
  528.7 4.2 fusion.65
  534.5 6.7 fusion.69
  546.4 8.3 fusion.40
  556.1 11.9 %fusion.82 = f32[2048,3072]{1,0:T(8,128)} fusion(bf16[288,3072]{1,0:T(8,128)(2,1)S(1)} %copy-done.6, bf16[288,2048]{1,0:T(8,128)(2,1)S(1)} %copy-done, f32[2048]{0:T(1024)S(1)} %convert_element_type.130, f32[288]{0:T(512)S(1)} %fusion.75), kind=kOutput, calls=%fused_computation.142 | convolution fusion | flops 3626237952 | bytes 28124288 | tf_op jit(solution)/shard_map/dot_general | solution.py:77
  568.7 46.0 %all-reduce.13 = (f32[2048]{0:T(1024)S(1)}, f32[512]{0:T(512)S(1)}) all-reduce(f32[2048]{0:T(1024)S(1)} %copy-done.40, f32[512]{0:T(512)S(1)} %copy-done.41), channel_id=3, replica_groups=mesh['dp'=1,'fsdp'=32] {'fsdp'}, use_global_device_ids=true, to_apply=%region_10.11.clone | all-reduce | flops 2560 | bytes 20480
  615.9 7.0 fusion.5
  622.9 124.4 %all-gather.14.cloned.1.call-done = f32[9216,2048]{1,0:T(8,128)} async-done(((f32[288,2048]{1,0:T(8,128)}), f32[9216,2048]{1,0:T(8,128)}) %all-gather.14.cloned.1.call-update) | async-done | bytes 75497488 | tf_op jit(solution)/shard_map/all_gather | solution.py:104
  747.3 131.0 %scatter_custom_fusion = f32[5120,2048]{1,0:T(8,128)} fusion(s32[9216]{0:T(1024)} %get-tuple-element.30, f32[9216,2048]{1,0:T(8,128)} %all-gather.14.cloned.1.call-done, f32[]{:T(128)} %constant.23.clone.1), kind=kCustom, calls=%fused_computation.3 | custom fusion | flops 18874368 | bytes 41943552 | tf_op jit(solution)/shard_map/scatter-add | solution.py:106
  878.3 21.7 %convert_element_type.170 = bf16[5120,2048]{1,0:T(8,128)(2,1)} convert(f32[5120,2048]{1,0:T(8,128)} %scatter_custom_fusion) | non-fusion elementwise | flops 10485760 | bytes 62914560 | tf_op jit(solution)/shard_map/convert_element_type | solution.py:106
  899.9 13.9 %reduce-scatter.12.cloned.1.call-done = f32[16,4096]{1,0:T(8,128)} async-done(((f32[512,4096]{1,0:T(8,128)}), f32[16,4096]{1,0:T(8,128)}) %reduce-scatter.12.cloned.1.call-update) | async-done | bytes 262160 | tf_op jit(solution)/shard_map/reduce_scatter | solution.py:107
  913.8 111.4 %reduce-scatter.14.cloned.1.call-done = f32[64,2048]{1,0:T(8,128)} async-done(((f32[2048,2048]{1,0:T(8,128)}), f32[64,2048]{1,0:T(8,128)}) %reduce-scatter.14.cloned.1.call-update) | async-done | bytes 524304 | tf_op jit(solution)/shard_map/reduce_scatter | solution.py:107
  1025.2 136.8 %reduce-scatter.8.cloned.1.call-done = f32[64,3072]{1,0:T(8,128)} async-done(((f32[2048,3072]{1,0:T(8,128)}), f32[64,3072]{1,0:T(8,128)}) %reduce-scatter.8.cloned.1.call-update) | async-done | bytes 786448 | tf_op jit(solution)/shard_map/reduce_scatter | solution.py:107
  (183 shorter events, 74.4 us)
Async XLA Ops:
  7.2 207.6 %all-gather.12.cloned.1.call-start = ((), (), s32[]{:S(2)}) async-start(), calls=%async_computation.9 | async-start | bytes 8650752 | tf_op jit(solution)/shard_map/all_gather | solution.py:102
  8.0 325.5 %reduce-scatter.6.cloned.1.call-start = ((), (), s32[]{:S(2)}) async-start(), calls=%async_computation.5 | async-start | bytes 38928384 | tf_op jit(solution)/shard_map/reduce_scatter | solution.py:101
  165.1 49.7 %copy-start.9 = (bf16[3,96,2048]{2,1,0:T(8,128)(2,1)S(1)}, bf16[3,96,2048]{2,1,0:T(8,128)(2,1)}, u32[]{:S(2)}) copy-start(bf16[3,96,2048]{2,1,0:T(8,128)(2,1)} %param.10) | copy-start | bytes 3538948
  165.1 228.1 %all-gather.10.cloned.1.call-start = ((), (), s32[]{:S(2)}) async-start(), calls=%async_computation.8 | async-start | bytes 12976128 | tf_op jit(solution)/shard_map/all_gather | solution.py:102
  165.9 267.7 %all-gather.6.cloned.1.call-start = ((), (), s32[]{:S(2)}) async-start(), calls=%async_computation.6 | async-start | bytes 2703360 | tf_op jit(solution)/shard_map/all_gather | solution.py:102
  166.6 309.2 %all-gather.8.cloned.1.call-start = ((), (), s32[]{:S(2)}) async-start(), calls=%async_computation.7 | async-start | bytes 4325376 | tf_op jit(solution)/shard_map/all_gather | solution.py:102
  167.2 580.1 %all-gather.14.cloned.1.call-start = ((), (), s32[]{:S(2)}) async-start(), calls=%async_computation.10 | async-start | bytes 77856768 | tf_op jit(solution)/shard_map/all_gather | solution.py:104
  212.2 8.6 copy-start.21
  212.2 8.6 copy-start.24
  407.5 26.1 %copy-start = (bf16[288,2048]{1,0:T(8,128)(2,1)S(1)}, bf16[288,2048]{1,0:T(8,128)(2,1)}, u32[]{:S(2)}) copy-start(bf16[288,2048]{1,0:T(8,128)(2,1)} %reduce-scatter.6.cloned.1.call-done) | copy-start | bytes 3538948
  480.7 7.9 copy-start.17
  485.8 5.2 copy-start.2
  485.8 7.5 copy-start.30
  486.3 6.9 copy-start.29
  498.6 2.8 copy-start.42
  499.7 4.5 copy-start.4
  501.3 2.9 copy-start.39
  516.2 8.0 copy-start.26
  516.2 8.0 copy-start.43
  528.6 371.3 %reduce-scatter.10.cloned.1.call-start = ((), (), s32[]{:S(2)}) async-start(), calls=%async_computation.12 | async-start | bytes 5406720 | tf_op jit(solution)/shard_map/reduce_scatter | solution.py:107
  532.9 380.9 %reduce-scatter.12.cloned.1.call-start = ((), (), s32[]{:S(2)}) async-start(), calls=%async_computation.13 | async-start | bytes 8650752 | tf_op jit(solution)/shard_map/reduce_scatter | solution.py:107
  541.2 484.0 %reduce-scatter.14.cloned.1.call-start = ((), (), s32[]{:S(2)}) async-start(), calls=%async_computation.14 | async-start | bytes 17301504 | tf_op jit(solution)/shard_map/reduce_scatter | solution.py:107
  554.7 607.4 %reduce-scatter.8.cloned.1.call-start = ((), (), s32[]{:S(2)}) async-start(), calls=%async_computation.11 | async-start | bytes 25952256 | tf_op jit(solution)/shard_map/reduce_scatter | solution.py:107
  568.0 47.9 %copy-start.8 = (bf16[3,96,16,128]{3,2,1,0:T(8,128)(2,1)S(1)}, bf16[3,96,16,128]{3,2,1,0:T(8,128)(2,1)}, u32[]{:S(2)}) copy-start(bf16[3,96,16,128]{3,2,1,0:T(8,128)(2,1)} %copy-done.7) | copy-start | bytes 3538948
  (32 other events, 43.1 us)
Sparse Core Ops, SparseCore 0:
  10.1 52.2 all-gather.11
  165.3 168.2 reduce-scatter.5
  335.6 57.5 all-gather.9
  395.2 38.4 all-gather.5
  435.6 40.1 all-gather.7
  528.7 218.5 all-gather.13
  751.4 74.0 reduce-scatter.9
  829.6 84.1 reduce-scatter.11
  918.1 107.0 reduce-scatter.13
  1029.4 132.5 reduce-scatter.7
where the time goes:
time: 1180 us; the launch traced here: 1170 us
  waiting for transfers between devices  618 us (52%)
  other arithmetic  196 us (17%)
  blocking collectives  141 us (12%)
  local copies, waits for them, and re-layouts  112 us (9%)
  matrix products  85.1 us (7%)
  between operations  15.1 us (1%)
    reduce_scatter x4, waiting for transfers between devices, device_step(): lax.psum_scatter(full_grad, 'fsdp', scatter_dimension=0, tiled=True)  262 us
    unnamed x3, blocking collectives  141 us
    scatter-add x1, other arithmetic, device_step(): jax.ops.segment_sum(all_grads, seg_ids, num_segments=vocab_dev)  131 us
    all_gather x1, waiting for transfers between devices, device_step(): all_grads = lax.all_gather(d_rows, 'fsdp', tiled=True)  124 us
    all_gather x4, waiting for transfers between devices, device_step(): lax.all_gather(shard_piece, 'fsdp', tiled=True)  117 us
    reduce_scatter x1, waiting for transfers between devices, device_step(): tok_rows = lax.psum_scatter(picked, 'fsdp', scatter_dimension=0, tiled=True)  111 us
    gather x1, local copies, waits for them, and re-layouts, device_step(): picked = jnp.take(emb_table, jnp.where(is_owned, local_ids, 0), axis=0)  78.5 us
    select_n x1, other arithmetic, device_step(): picked = jnp.where(is_owned[:, None], picked, jnp.zeros((), picked.dtype))  25.6 us
  transfers between devices with their start and end apart: 10, of which 8 were waited for; matrix products, arithmetic and copies ran while one was open for 29% of the time, Pallas kernels for 0%

commit v1 on v0

v1 whole, which is shorter than its diff:
```python
import functools
import math
import jax
import jax.numpy as jnp
from jax import lax
from jax.experimental import pallas as pl
from jax.experimental.pallas import tpu as pltpu
from jax.sharding import PartitionSpec as P

NOPE_DIM = 128
ROPE_DIM = 64
VALUE_DIM = 128
ROPE_THETA = 50000.0
RMS_EPS = 1e-6
ATTN_SCALE = (NOPE_DIM + ROPE_DIM) ** -0.5 * (0.1 * math.log(32.0) + 1.0) ** 2
ROW_DIMS = (((0,), (0,)), ((), ()))
COL_DIMS = (((1,), (1,)), ((), ()))
LANES = 128


def weight_grads_kernel(widths, up_rows, up_cut, x_ref, d_query_ref, d_down_ref, mix_ref, d_out_ref, latent_ref, d_up_ref, out_ref):
    q_width, o_width, up_cols, c_width, spare_width = widths

    def grad(rows_ref, cols):
        return lax.dot_general(rows_ref[...], cols, ROW_DIMS, preferred_element_type=jnp.float32)

    out_ref[:, :q_width] = grad(x_ref, d_query_ref[...])
    at = q_width
    out_ref[:, at:at + o_width] = grad(mix_ref, d_out_ref[...])
    at += o_width
    for cut in range(up_cut):
        piece = lax.dot_general(latent_ref[0], d_up_ref[:, cut * up_cols:(cut + 1) * up_cols], ROW_DIMS, preferred_element_type=jnp.float32)
        for d in range(piece.shape[0] // up_rows):
            low = (d * up_cut + cut) * up_rows
            out_ref[low:low + up_rows, at:at + up_cols] = piece[d * up_rows:(d + 1) * up_rows]
    at += up_cols
    tail = grad(x_ref, d_down_ref[...])
    out_ref[:, at:] = jnp.concatenate([tail, jnp.zeros((tail.shape[0], spare_width), jnp.float32)], axis=1)


def weight_grads(up_rows, up_cut, normed, d_query, d_down, mix_rows, d_out, latent, d_up):
    toks, rows = normed.shape
    widths = (d_query.shape[1], d_out.shape[1], d_up.shape[1] // up_cut, d_down.shape[1])
    widths += (-sum(widths) % 1024,)
    block = min(256, rows)
    steps = rows // block
    kv_block = latent.shape[1] // steps
    latent = latent.reshape(toks, steps, kv_block).transpose(1, 0, 2)
    whole = lambda a: pl.BlockSpec(a.shape, lambda i: (0, 0))
    cols = pl.BlockSpec((toks, block), lambda i: (0, i))
    return pl.pallas_call(
        functools.partial(weight_grads_kernel, widths, up_rows, up_cut),
        out_shape=jax.ShapeDtypeStruct((rows, sum(widths)), jnp.float32),
        grid=(steps,),
        in_specs=[cols, whole(d_query), whole(d_down), cols, whole(d_out), pl.BlockSpec((1, toks, kv_block), lambda i: (i, 0, 0)), whole(d_up)],
        out_specs=pl.BlockSpec((block, sum(widths)), lambda i: (i, 0)),
        compiler_params=pltpu.CompilerParams(vmem_limit_bytes=48_000_000),
        cost_estimate=pl.CostEstimate(flops=2 * toks * rows * sum(widths), bytes_accessed=4 * rows * sum(widths), transcendentals=0),
        name='weight_grads',
    )(normed, d_query, d_down, mix_rows, d_out, latent, d_up)


def rms_scale(in_vals, gain_vec):
    vals_f32 = in_vals.astype(jnp.float32)
    inv_rms = lax.rsqrt(jnp.mean(vals_f32 * vals_f32, axis=-1, keepdims=True) + RMS_EPS)
    return (vals_f32 * inv_rms * gain_vec).astype(jnp.bfloat16)


def rope_tables(seq_len):
    positions = jnp.arange(seq_len, dtype=jnp.float32)
    inv_freq = ROPE_THETA ** (-2.0 * jnp.arange(ROPE_DIM // 2, dtype=jnp.float32) / ROPE_DIM)
    rot_angle = positions[:, None] * inv_freq[None, :]
    rot_angle = jnp.concatenate([rot_angle, rot_angle], axis=-1)
    return jnp.cos(rot_angle), jnp.sin(rot_angle)


def apply_rope(in_vals, cos_tab, sin_tab):
    half_dim = ROPE_DIM // 2
    vals_f32 = in_vals.astype(jnp.float32)
    turned = jnp.concatenate([-vals_f32[..., half_dim:], vals_f32[..., :half_dim]], axis=-1)
    return (vals_f32 * cos_tab + turned * sin_tab).astype(jnp.bfloat16)


def attend_local(q_proj, pe_raw, kv_up):
    seq_len = q_proj.shape[1]
    cos_tab, sin_tab = rope_tables(seq_len)
    q_rot = apply_rope(q_proj[..., NOPE_DIM:], cos_tab[:, None, :], sin_tab[:, None, :])
    k_rot = apply_rope(pe_raw, cos_tab, sin_tab)
    scores = jnp.einsum('bshd,bthd->bhst', q_proj[..., :NOPE_DIM], kv_up[..., :NOPE_DIM], preferred_element_type=jnp.float32)
    scores = scores + jnp.einsum('bshd,btd->bhst', q_rot, k_rot, preferred_element_type=jnp.float32)
    positions = jnp.arange(seq_len)
    causal = positions[:, None] >= positions[None, :]
    scores = jnp.where(causal, scores * ATTN_SCALE, -1e30)
    attn_probs = jax.nn.softmax(scores, axis=-1).astype(jnp.bfloat16)
    attn_mix = jnp.einsum('bhst,bthd->bshd', attn_probs, kv_up[..., NOPE_DIM:], preferred_element_type=jnp.float32)
    return attn_mix.astype(jnp.bfloat16)


def solution(mesh):
    tok_spec = P(('dp', 'fsdp'), None)
    seq_spec = P(('dp', 'fsdp'), None, None)
    part_vec = P(('dp', 'fsdp'))
    vec_spec = P('fsdp')
    mat_spec = P('fsdp', None)
    n = mesh.shape['fsdp']

    def device_step(tok_ids, grad_out, emb_table, norm_gain, w_query, w_kv_down, kv_gain, w_kv_up, w_out):
        seq_count, seq_len = tok_ids.shape
        vocab, d_model = emb_table.shape
        toks = seq_count * seq_len
        me = lax.axis_index('fsdp')
        d_rows_w, q_width = w_query.shape
        c_width = w_kv_down.shape[1]
        up_rows, up_width = w_kv_up.shape
        kv_rank = up_rows * n
        gain_len, kv_gain_len = norm_gain.shape[0], kv_gain.shape[0]
        up_cut = d_rows_w // up_rows
        up_cols = up_width // up_cut
        grad_rows = grad_out.reshape(toks, d_model)

        o_width = w_out.shape[1]
        o_end = q_width + o_width
        up_end = o_end + up_cols
        down_end = up_end + c_width
        w_query_full, w_down_full, w_up_full, w_out_full = (lax.all_gather(shard, 'fsdp', tiled=True) for shard in (w_query, w_kv_down, w_kv_up, w_out))

        def to_all(parts):
            return lax.all_gather(jnp.concatenate(parts), 'fsdp')

        padded = -(-toks // LANES) * LANES
        ids_f32 = jnp.concatenate([tok_ids.reshape(toks).astype(jnp.float32), jnp.zeros((padded - toks,), jnp.float32)])
        spread_all = to_all([ids_f32, norm_gain.astype(jnp.float32), kv_gain.astype(jnp.float32)])
        all_ids = spread_all[:, :toks].reshape(n * toks).astype(jnp.int32)
        gain_vec = spread_all[:, padded:padded + gain_len].reshape(n * gain_len)
        kv_gain_vec = spread_all[:, padded + gain_len:padded + gain_len + kv_gain_len].reshape(n * kv_gain_len)

        local_ids = all_ids - me * vocab
        is_owned = (local_ids >= 0) & (local_ids < vocab)
        picked = jnp.take(emb_table, jnp.where(is_owned, local_ids, 0), axis=0)
        picked = jnp.where(is_owned[:, None], picked, jnp.zeros((), picked.dtype))
        w_query_full, w_down_full, w_up_full, w_out_full, to_send = lax.optimization_barrier((w_query_full, w_down_full, w_up_full, w_out_full, picked))
        got = lax.psum_scatter(to_send, 'fsdp', scatter_dimension=0, tiled=True)
        got, late_grads = lax.optimization_barrier((got, grad_rows))
        all_d_out = lax.all_gather(late_grads, 'fsdp', tiled=True)
        rows_f32 = got.astype(jnp.float32)

        normed, norm_pull = jax.vjp(rms_scale, rows_f32, gain_vec)
        kv_down = jnp.dot(normed, w_down_full, preferred_element_type=jnp.float32).astype(jnp.bfloat16)
        q_proj = jnp.dot(normed, w_query_full, preferred_element_type=jnp.float32).astype(jnp.bfloat16)
        latent, latent_pull = jax.vjp(rms_scale, kv_down[:, :kv_rank], kv_gain_vec)
        kv_up = jnp.dot(latent, w_up_full, preferred_element_type=jnp.float32).astype(jnp.bfloat16)
        attn_mix, attn_pull = jax.vjp(attend_local, q_proj.reshape(seq_count, seq_len, -1, NOPE_DIM + ROPE_DIM), kv_down[:, kv_rank:].reshape(seq_count, seq_len, ROPE_DIM), kv_up.reshape(seq_count, seq_len, -1, NOPE_DIM + VALUE_DIM))
        mix_rows = attn_mix.reshape(toks, -1)
        out_f32 = rows_f32 + jnp.dot(mix_rows, w_out_full, preferred_element_type=jnp.float32)
        d_mix = lax.dot_general(grad_rows, w_out_full, COL_DIMS, preferred_element_type=jnp.float32).astype(jnp.bfloat16)
        d_query, d_pe, d_up = attn_pull(d_mix.reshape(attn_mix.shape))
        d_query = d_query.reshape(toks, -1)
        d_up = d_up.reshape(toks, -1)
        d_latent = lax.dot_general(d_up, w_up_full, COL_DIMS, preferred_element_type=jnp.float32).astype(jnp.bfloat16)
        d_ckv, d_kv_gain = latent_pull(d_latent)
        d_down = jnp.concatenate([d_ckv, d_pe.reshape(toks, ROPE_DIM)], axis=1)
        d_normed = lax.dot_general(d_query, w_query_full, COL_DIMS, preferred_element_type=jnp.float32)
        d_normed = d_normed + lax.dot_general(d_down, w_down_full, COL_DIMS, preferred_element_type=jnp.float32)
        d_normed = d_normed.astype(jnp.bfloat16)
        _, d_gain = norm_pull(d_normed)
        late_normed, all_d_out = lax.optimization_barrier((d_normed, all_d_out))
        all_d_normed = lax.all_gather(late_normed, 'fsdp', tiled=True)
        inv_rms = lax.rsqrt(jnp.mean(rows_f32 * rows_f32, axis=-1) + RMS_EPS)
        pull = inv_rms * inv_rms * inv_rms * jnp.mean(rows_f32 * d_normed.astype(jnp.float32) * gain_vec, axis=-1)
        pad_toks = jnp.zeros((padded - toks,), jnp.float32)
        scales = to_all([inv_rms, pad_toks, pull, pad_toks])

        d_w_cat = weight_grads(up_rows, up_cut, normed, d_query, d_down, mix_rows, grad_rows, latent, d_up)
        small = lax.psum_scatter(jnp.concatenate([d_gain.reshape(n, gain_len), d_kv_gain.reshape(n, kv_gain_len)], axis=1).reshape(-1), 'fsdp', scatter_dimension=0, tiled=True)
        d_w_cat, all_d_normed, scales, small = lax.optimization_barrier((d_w_cat, all_d_normed, scales, small))
        d_w_shard = lax.psum_scatter(d_w_cat, 'fsdp', scatter_dimension=0, tiled=True)

        all_inv = scales[:, :toks].reshape(n * toks, 1)
        all_pull = scales[:, padded:padded + toks].reshape(n * toks, 1)
        token_grads = all_d_normed.astype(jnp.float32) * gain_vec * all_inv - picked.astype(jnp.float32) * all_pull + all_d_out.astype(jnp.float32)
        grad_table = jax.ops.segment_sum(token_grads, jnp.where(is_owned, local_ids, vocab), num_segments=vocab).astype(jnp.bfloat16)

        d_w_up_shard = d_w_shard[:, o_end:up_end].reshape(up_cut, up_rows, up_cols).transpose(1, 0, 2).reshape(up_rows, up_width)
        return (
            out_f32.astype(jnp.bfloat16).reshape(seq_count, seq_len, d_model),
            grad_table,
            small[:gain_len],
            d_w_shard[:, :q_width],
            d_w_shard[:, up_end:down_end],
            small[gain_len:gain_len + kv_gain_len],
            d_w_up_shard,
            d_w_shard[:, q_width:o_end],
        )

    return jax.shard_map(device_step, mesh=mesh, in_specs=(tok_spec, seq_spec, mat_spec, vec_spec, mat_spec, mat_spec, vec_spec, mat_spec, mat_spec), out_specs=(seq_spec, tok_spec, part_vec, tok_spec, tok_spec, part_vec, tok_spec, tok_spec), check_vma=False)
```

time: 1180 us -> 880 us (0.75)
  waiting for transfers between devices: 618 us -> 261 us
  other arithmetic: 196 us -> 258 us
  matrix products: 85.1 us -> 51.7 us
  Pallas kernels: 0 us -> 25.2 us
  local copies, waits for them, and re-layouts: 112 us -> 132 us
  blocking collectives: 141 us -> 129 us
    reduce_scatter x5 -> x2, waiting for transfers between devices: 374 us -> 186 us  [the longest x1 173 us: device_step(): got = lax.psum_scatter(to_send, 'fsdp', scatter_dimension=0, tiled=True)]
    all_gather x5 -> x6, waiting for transfers between devices: 242 us -> 71.6 us  [the longest x1 36.9 us: device_step(): all_d_out = lax.all_gather(late_grads, 'fsdp', tiled=True)]
    add x1, other arithmetic: 2.23 us -> 60.9 us  [device_step(): all_d_normed.astype(jnp.float32) * gain_vec * all_inv]
    unnamed x3 -> x2, blocking collectives: 141 us -> 101 us
    dot_general x12 -> x8, matrix products: 73.6 us -> 40.7 us  [the longest x1 7.63 us: device_step(): lax.dot_general(d_query, w_query_full, COL_DIMS, preferred_element_type=j...]
    all_gather x0 -> x1, blocking collectives: none -> 28 us  [to_all(): return lax.all_gather(jnp.concatenate(parts), 'fsdp')]
    pallas_call x0 -> x1, Pallas kernels: none -> 25.2 us  [weight_grads(): pl.pallas_call(functools.partial(weight_grads_kernel, widths, up_rows, up...]
    convert_element_type x3 -> x6, other arithmetic: 21.7 us -> 25.1 us  [the longest x1 21.7 us: device_step(): jax.ops.segment_sum(token_grads, jnp.where(is_owned, local_ids, vocab), n...]
  transfers between devices with their start and end apart: 10 -> 8, of which waited for: 8 -> 4; matrix products, arithmetic and copies ran while one was open for 29% -> 48% of each run, Pallas kernels for 0% -> 3%
where the time goes in v1:
time: 880 us; the launch traced here: 873 us
  waiting for transfers between devices  261 us (30%)
  other arithmetic  258 us (29%)
  local copies, waits for them, and re-layouts  132 us (15%)
  blocking collectives  129 us (15%)
  matrix products  51.7 us (6%)
  Pallas kernels  25.2 us (3%)
  between operations  15.4 us (2%)
    reduce_scatter x1, waiting for transfers between devices, device_step(): got = lax.psum_scatter(to_send, 'fsdp', scatter_dimension=0, tiled=True)  173 us
    scatter-add x1, other arithmetic, device_step(): jax.ops.segment_sum(token_grads, jnp.where(is_owned, local_ids, vocab), n...  131 us
    unnamed x2, blocking collectives  101 us
    gather x1, local copies, waits for them, and re-layouts, device_step(): picked = jnp.take(emb_table, jnp.where(is_owned, local_ids, 0), axis=0)  78.5 us
    add x1, other arithmetic, device_step(): all_d_normed.astype(jnp.float32) * gain_vec * all_inv  60.9 us
    all_gather x1, waiting for transfers between devices, device_step(): all_d_out = lax.all_gather(late_grads, 'fsdp', tiled=True)  36.9 us
    all_gather x4, waiting for transfers between devices, device_step(): lax.all_gather(shard, 'fsdp', tiled=True)  34.7 us
    all_gather x1, blocking collectives, to_all(): return lax.all_gather(jnp.concatenate(parts), 'fsdp')  28 us
  transfers between devices with their start and end apart: 8, of which 4 were waited for; matrix products, arithmetic and copies ran while one was open for 48% of the time, Pallas kernels for 3%

profile of v1, /device:TPU:97, one launch (start us, length us, event | category | flops | bytes accessed | tf_op | source)
XLA Modules:
  0.0 873.1 jit_solution(8906041444445457791)
XLA Ops:
  13.1 50.3 %all-reduce.8 = f32[14848]{0:T(1024)S(1)} all-reduce(f32[14848]{0:T(1024)S(1)} %maximum_dynamic-update-slice_fusion), channel_id=2, replica_groups=mesh['dp'=1,'fsdp'=32] {'fsdp'}, use_global_device_ids=true, to_apply=%add.8 | all-reduce | flops 14848 | bytes 118784
  64.4 78.5 %gather_fusion = bf16[9216,2048]{1,0:T(8,128)(2,1)} fusion(bf16[5120,2048]{1,0:T(8,128)(2,1)} %param.11, s32[9216]{0:T(1024)S(1)} %broadcast_clamp_fusion), kind=kCustom, calls=%fused_computation | custom fusion | bytes 75534336 | tf_op jit(solution)/shard_map/jit(_take)/gather | solution.py:139
  142.9 25.9 %select_select_fusion = bf16[9216,2048]{1,0:T(8,128)(2,1)} fusion(bf16[9216,2048]{1,0:T(8,128)(2,1)} %gather_fusion, pred[9216]{0:T(1024)(128)(4,1)S(1)} %get-tuple-element.57, pred[9216]{0:T(1024)(128)(4,1)S(1)} %get-tuple-element.56), kind=kLoop, calls=%fused_computation.3 | loop fusion | flops 37748736 | bytes 75515904 | tf_op jit(solution)/shard_map/jit(_where)/select_n | solution.py:140
  168.9 34.6 %all-gather.10.cloned.1.call-done = bf16[2048,3072]{1,0:T(8,128)(2,1)} async-done(((bf16[64,3072]{1,0:T(8,128)(2,1)}), bf16[2048,3072]{1,0:T(8,128)(2,1)}) %all-gather.10.cloned.1.call-update) | async-done | bytes 12582928 | tf_op jit(solution)/shard_map/all_gather | solution.py:125
  203.7 172.8 %reduce-scatter.3.cloned.1.call-done = bf16[288,2048]{1,0:T(8,128)(2,1)} async-done(((bf16[9216,2048]{1,0:T(8,128)(2,1)}), bf16[288,2048]{1,0:T(8,128)(2,1)}) %reduce-scatter.3.cloned.1.call-update) | async-done | bytes 1179664 | tf_op jit(solution)/shard_map/reduce_scatter | solution.py:142
  380.3 6.2 fusion.37
  388.6 5.1 convolution_convert_fusion.1
  393.8 5.1 reshape.259
  401.8 2.8 convolution_convert_fusion.9
  408.3 3.7 convolution_convert_fusion
  438.3 2.8 copy.74
  441.0 3.9 reshape.263.d_query_ref
  445.0 5.1 fusion.55
  450.3 7.6 fusion.79
  458.0 3.1 fusion.9
  461.1 36.9 %all-gather.18.cloned.1.call-done = bf16[9216,2048]{1,0:T(8,128)(2,1)} async-done(((bf16[288,2048]{1,0:T(8,128)(2,1)}), bf16[9216,2048]{1,0:T(8,128)(2,1)}) %all-gather.18.cloned.1.call-update) | async-done | bytes 37748752 | tf_op jit(solution)/shard_map/all_gather | solution.py:144
  513.1 28.0 %all-gather.2 = f32[32,1,768]{2,1,0:T(1,128)S(1)} all-gather(f32[1,1,768]{2,1,0:T(1,128)S(1)} %reshape.293), channel_id=3, replica_groups=mesh['dp'=1,'fsdp'=32] {'fsdp'}, dimensions={0}, use_global_device_ids=true | all-gather | bytes 101376 | tf_op jit(solution)/shard_map/all_gather | solution.py:128
  541.8 51.1 %all-reduce.9 = f32[2560]{0:T(1024)} all-reduce(f32[2560]{0:T(1024)} %reshape.269), channel_id=5, replica_groups=mesh['dp'=1,'fsdp'=32] {'fsdp'}, use_global_device_ids=true, to_apply=%region_10.11.clone | all-reduce | flops 2560 | bytes 20480
  597.3 25.2 %weight_grads.1 = f32[2048,7168]{1,0:T(8,128)} custom-call(bf16[288,2048]{1,0:T(8,128)(2,1)S(1)} %copy-done.3, bf16[288,3072]{1,0:T(8,128)(2,1)S(1)} %reshape.263.d_query_ref, bf16[288,576]{1,0:T(8,128)(2,1)S(1)} %pad_maximum_fusion.d_down_ref, bf16[288,2048]{1,0:T(8,128)(2,1)S(1)} %bitcast.121, bf16[288,2048]{1,0:T(8,128)(2,1)S(1)} %bitcast.120, ...), custom_call_target="tpu_custom_call" | custom-call | flops 8455716864 | bytes 58720256 | tf_op jit(solution)/shard_map/weight_grads/pallas_call | solution.py:51
  624.1 7.0 fusion.4
  632.0 60.9 %convert_add_fusion = f32[9216,2048]{1,0:T(8,128)} fusion(bf16[9216,2048]{1,0:T(8,128)(2,1)} %all-gather.18.cloned.1.call-done, bf16[9216,2048]{1,0:T(8,128)(2,1)} %all-gather.20.cloned.1.call-done, f32[9216]{0:T(1024)S(1)} %mul.314, f32[9216]{0:T(1024)S(1)} %mul.311, f32[2048]{0:T(1024)S(1)} %copy-done.40, bf16[9216,2048]{1,0:T(8,128)(2,1)} %gather_fusion, ...), kind=kLoop, calls=%fused_computation.2 | loop fusion | flops 188743680 | bytes 188844032 | tf_op jit(solution)/shard_map/add | solution.py:180
  692.8 131.0 %scatter_custom_fusion = f32[5120,2048]{1,0:T(8,128)} fusion(s32[9216]{0:T(1024)} %bitcast.142, f32[9216,2048]{1,0:T(8,128)} %convert_add_fusion, f32[]{:T(128)} %constant.17.clone.1), kind=kCustom, calls=%fused_computation.4 | custom fusion | flops 18874368 | bytes 41943552 | tf_op jit(solution)/shard_map/scatter-add | solution.py:181
  823.8 21.7 %convert_element_type.213 = bf16[5120,2048]{1,0:T(8,128)(2,1)} convert(f32[5120,2048]{1,0:T(8,128)} %scatter_custom_fusion) | non-fusion elementwise | flops 10485760 | bytes 62914560 | tf_op jit(solution)/shard_map/convert_element_type | solution.py:181
  845.5 13.3 %reduce-scatter.5.cloned.1.call-done = f32[64,7168]{1,0:T(8,128)} async-done(((f32[2048,7168]{1,0:T(8,128)}), f32[64,7168]{1,0:T(8,128)}) %reduce-scatter.5.cloned.1.call-update) | async-done | bytes 1835024 | tf_op jit(solution)/shard_map/reduce_scatter | solution.py:176
  (226 shorter events, 75.0 us)
Async XLA Ops:
  7.2 161.6 %all-gather.12.cloned.1.call-start = ((), (), s32[]{:S(2)}) async-start(), calls=%async_computation.3 | async-start | bytes 2703360 | tf_op jit(solution)/shard_map/all_gather | solution.py:125
  8.0 160.9 %all-gather.14.cloned.1.call-start = ((), (), s32[]{:S(2)}) async-start(), calls=%async_computation.4 | async-start | bytes 4325376 | tf_op jit(solution)/shard_map/all_gather | solution.py:125
  8.8 160.1 %all-gather.16.cloned.1.call-start = ((), (), s32[]{:S(2)}) async-start(), calls=%async_computation.5 | async-start | bytes 8650752 | tf_op jit(solution)/shard_map/all_gather | solution.py:125
  9.6 193.9 %all-gather.10.cloned.1.call-start = ((), (), s32[]{:S(2)}) async-start(), calls=%async_computation.2 | async-start | bytes 12976128 | tf_op jit(solution)/shard_map/all_gather | solution.py:125
  10.2 366.2 %reduce-scatter.3.cloned.1.call-start = ((), (), s32[]{:S(2)}) async-start(), calls=%async_computation.6 | async-start | bytes 38928384 | tf_op jit(solution)/shard_map/reduce_scatter | solution.py:142
  142.9 25.9 %copy-start.36 = (pred[9216]{0:T(1024)(128)(4,1)}, pred[9216]{0:T(1024)(128)(4,1)S(1)}, u32[]{:S(2)}) copy-start(pred[9216]{0:T(1024)(128)(4,1)S(1)} %get-tuple-element.57) | copy-start | bytes 27652
  168.8 211.5 %copy-start = (bf16[3,96,2048]{2,1,0:T(8,128)(2,1)S(1)}, bf16[3,96,2048]{2,1,0:T(8,128)(2,1)}, u32[]{:S(2)}) copy-start(bf16[3,96,2048]{2,1,0:T(8,128)(2,1)} %param.10) | copy-start | bytes 3538948
  203.6 294.5 %all-gather.18.cloned.1.call-start = ((), (), s32[]{:S(2)}) async-start(), calls=%async_computation.7 | async-start | bytes 38928384 | tf_op jit(solution)/shard_map/all_gather | solution.py:144
  376.5 246.0 %all-gather.20.cloned.1.call-start = ((), (), s32[]{:S(2)}) async-start(), calls=%async_computation.8 | async-start | bytes 38928384 | tf_op jit(solution)/shard_map/all_gather | solution.py:167
  377.5 9.0 %copy-start.22 = (f32[96,64]{1,0:T(8,128)}, f32[96,64]{1,0:T(8,128)S(1)}, u32[]{:S(2)}) copy-start(f32[96,64]{1,0:T(8,128)S(1)} %get-tuple-element.52) | copy-start | bytes 73732
  377.5 9.0 %copy-start.25 = (f32[96,64]{1,0:T(8,128)}, f32[96,64]{1,0:T(8,128)S(1)}, u32[]{:S(2)}) copy-start(f32[96,64]{1,0:T(8,128)S(1)} %get-tuple-element.53) | copy-start | bytes 73732
  379.0 9.2 %copy-start.38 = (f32[2048]{0:T(1024)}, f32[2048]{0:T(1024)S(1)}, u32[]{:S(2)}) copy-start(f32[2048]{0:T(1024)S(1)} %mul.261) | copy-start | bytes 24580
  380.3 8.3 copy-start.55
  388.6 13.2 %copy-start.2 = (bf16[288,2048]{1,0:T(8,128)(2,1)}, bf16[288,2048]{1,0:T(8,128)(2,1)S(1)}, u32[]{:S(2)}) copy-start(bf16[288,2048]{1,0:T(8,128)(2,1)S(1)} %fusion.5.x_ref) | copy-start | bytes 3538948
  418.3 9.9 %copy-start.34 = (f32[3,16,96]{2,1,0:T(8,128)}, f32[3,16,96]{2,1,0:T(8,128)S(1)}, u32[]{:S(2)}) copy-start(f32[3,16,96]{2,1,0:T(8,128)S(1)} %get-tuple-element.38) | copy-start | bytes 55300
  418.8 9.3 %copy-start.32 = (f32[3,16,96]{2,1,0:T(8,128)}, f32[3,16,96]{2,1,0:T(8,128)S(1)}, u32[]{:S(2)}) copy-start(f32[3,16,96]{2,1,0:T(8,128)S(1)} %fusion.32) | copy-start | bytes 55300
  450.3 7.7 copy-start.21
  450.3 7.7 copy-start.10
  450.3 7.7 copy-start.30
  458.0 40.2 %copy-start.17 = (bf16[288,512]{1,0:T(8,128)(2,1)S(1)}, bf16[288,512]{1,0:T(8,128)(2,1)}, u32[]{:S(2)}) copy-start(bf16[288,512]{1,0:T(8,128)(2,1)} %copy-done.16) | copy-start | bytes 884740
  498.1 360.7 %reduce-scatter.5.cloned.1.call-start = ((), (), s32[]{:S(2)}) async-start(), calls=%async_computation.9 | async-start | bytes 60555264 | tf_op jit(solution)/shard_map/reduce_scatter | solution.py:176
  593.7 37.5 %copy-start.57 = (f32[80]{0:T(128)}, f32[80]{0:T(128)S(1)}, u32[]{:S(2)}) copy-start(f32[80]{0:T(128)S(1)} %dynamic-slice) | copy-start | bytes 964
  624.1 7.8 copy-start.37
  624.1 7.8 copy-start.40
  (42 other events, 121.3 us)
Sparse Core Ops, SparseCore 0:
  10.1 43.4 all-gather.11
  55.7 40.1 all-gather.13
  98.0 46.6 all-gather.15
  146.6 56.8 all-gather.9
  207.2 169.2 reduce-scatter.2
  378.3 119.6 all-gather.17
  500.2 120.6 all-gather.19
  624.6 234.1 reduce-scatter.4
